TPU v7x, 32 devices: a whole 2x2x4 slice. The times are simulated.
32 devices in a mesh: section: 8 (over z, x), expert: 4 (over y, core).
Axes of the slice: x: 2, y: 2, z: 4, core: 2. Of those that a mesh axis runs over, the one named last changes fastest.
Arguments:
- tokens: bfloat16 [16, 32, 768], P(None, 'expert'), may hold values from -6 to 6
- route_ids: int32 [8, 16, 32, 2], P('section'), may hold values from 0 to 3, all different within a row; in each aligned block of 8 rows (0 to 7, 8 to 15, ..., all dimensions but the last counted through in order) at most 8 rows name the same one
- router: bfloat16 [8, 768, 4], P('section'), may hold values from -0.21875 to 0.21875
- norm_gain: float32 [8, 768], P('section'), may hold values from 0.1 to 1.9
- weight_in: bfloat16 [8, 4, 768, 3072], P('section', 'expert'), may hold values from -0.21875 to 0.21875
- weight_out: bfloat16 [8, 4, 3072, 768], P('section', 'expert'), may hold values from -0.109375 to 0.109375
Outputs:
- layer_states: bfloat16 [8, 16, 32, 768], P('section', None, 'expert')
Inputs may be any that keep to these rules, and one draw needn't show every extreme that they name: `route_ids`: each row names two different experts. In each aligned block of 8 rows (the tokens of one micro-batch on one index of the expert axis) no expert is named by more than 8 rows, and in some blocks one expert is named by exactly 8.
All inputs are finite; a program needn't handle non-finite values.
Results may differ from a plain program's by a relative error of at most 0.028.
Values may be sent and summed in bfloat16 or wider, within the bound.
No kernel may reach another device: no remote copies, remote signals or barrier semaphores. Data moves between devices by JAX's collectives and lax.ppermute only.
A program may use at most 64 MiB of HBM per device.

v0:
```python
import jax
import jax.numpy as jnp
from jax import lax
from jax.sharding import PartitionSpec as P

epsilon = 1e-06


def from_behind(block, axis, distance):
    devices = range(lax.axis_size(axis))
    route = [(i - distance, i) for i in devices if i - distance in devices]
    return lax.ppermute(block, axis, route)


def slot_targets(route_block, experts, capacity):
    owners = route_block.shape[0]
    assigned = route_block.reshape(owners, -1)
    onehot = (assigned[:, :, None] == jnp.arange(experts, dtype=jnp.int32)[None, None, :]).astype(
        jnp.int32
    )
    earlier = jnp.cumsum(onehot, axis=1) - onehot
    position = jnp.sum(onehot * earlier, axis=2)
    return (assigned * capacity + position).reshape(route_block.shape)


def body(tokens, route_ids, router, norm_gain, weight_in, weight_out):
    groups = lax.axis_size("expert")
    sections = lax.axis_size("section")
    section_index = lax.axis_index("section")
    member = lax.axis_index("expert")
    micro_count, tok_rows, features = tokens.shape
    experts = router.shape[2]
    capacity = 4 * tok_rows // experts
    slot_total = experts * capacity
    routes_all = route_ids[0]
    router_block = router[0]
    gain_row = norm_gain[0]
    expert_in = weight_in[0, 0]
    expert_out = weight_out[0, 0]
    columns = jnp.arange(slot_total, dtype=jnp.int32)
    expert_range = jnp.arange(experts, dtype=jnp.int32)
    contract_rows = (((0,), (0,)), ((), ()))

    def apply_expert(received):
        flattened = received.reshape(-1, features)
        hidden = jax.nn.relu(
            jnp.dot(flattened, expert_in, preferred_element_type=jnp.float32)
        ).astype(jnp.bfloat16)
        produced = jnp.dot(hidden, expert_out, preferred_element_type=jnp.float32).astype(
            jnp.bfloat16
        )
        return lax.all_to_all(
            produced.reshape(received.shape), "expert", split_axis=0, concat_axis=0, tiled=True
        )

    def apply_layer(current, route_block):
        stream = current.astype(jnp.float32)
        inverse = lax.rsqrt(jnp.mean(stream * stream, axis=-1, keepdims=True) + epsilon)
        normed = (stream * inverse * gain_row).astype(jnp.bfloat16)
        logits = jnp.dot(normed, router_block, preferred_element_type=jnp.float32)
        owners_block = route_block.reshape(groups, tok_rows, 2)
        targets = slot_targets(owners_block, experts, capacity)
        own_targets = lax.dynamic_index_in_dim(targets, member, 0, keepdims=False)
        own_experts = lax.dynamic_index_in_dim(owners_block, member, 0, keepdims=False)
        selector = (own_targets[:, :, None] == columns[None, None, :]).astype(jnp.bfloat16)
        owner_base = jnp.arange(groups, dtype=jnp.int32)[:, None, None] * capacity
        place = jnp.where(owners_block == member, owner_base + targets - member * capacity, -1)
        receive_columns = jnp.arange(groups * capacity, dtype=jnp.int32)
        picker = jnp.sum(
            (place[..., None] == receive_columns[None, None, None, :]).astype(jnp.bfloat16), axis=2
        )
        picker = picker.reshape(groups * tok_rows, groups * capacity)
        collected = lax.dot_general(
            picker,
            lax.all_gather(normed, "expert", axis=0, tiled=True),
            contract_rows,
            preferred_element_type=jnp.float32,
        )
        returned = apply_expert(collected.astype(jnp.bfloat16).reshape(groups, capacity, features))
        picked = jnp.einsum(
            "tkr,rd->tkd",
            selector,
            returned.reshape(slot_total, features),
            preferred_element_type=jnp.float32,
        )
        chosen = (own_experts[:, :, None] == expert_range[None, None, :]).astype(jnp.float32)
        gate_values = jax.nn.sigmoid(jnp.sum(chosen * logits[:, None, :], axis=2))
        mixed = stream + gate_values[:, 0:1] * picked[:, 0] + gate_values[:, 1:2] * picked[:, 1]
        return mixed.astype(jnp.bfloat16)

    def relay_turn(counter, state_pair):
        received, states = state_pair
        offset_turn = counter - section_index
        active_turn = jnp.logical_and(offset_turn >= 0, offset_turn < micro_count)
        micro_index = jnp.clip(offset_turn, 0, micro_count - 1)
        entering = lax.dynamic_index_in_dim(tokens, micro_index, 0, keepdims=False)
        current = jnp.where(section_index == 0, entering, received)
        route_block = lax.dynamic_index_in_dim(routes_all, micro_index, 0, keepdims=False)
        result = apply_layer(current, route_block)
        previous = lax.dynamic_index_in_dim(states, micro_index, 0, keepdims=False)
        states = lax.dynamic_update_index_in_dim(
            states, jnp.where(active_turn, result, previous), micro_index, 0
        )
        received = from_behind(result, "section", 1)
        return (received, states)

    initial = (
        jnp.zeros((tok_rows, features), jnp.bfloat16),
        jnp.zeros((micro_count, tok_rows, features), jnp.bfloat16),
    )
    leftover, states = lax.fori_loop(0, micro_count + sections - 1, relay_turn, initial)
    return states[None]


def solution(mesh):
    placed = (
        P(None, "expert", None),
        P("section", None, None, None),
        P("section", None, None),
        P("section", None),
        P("section", "expert", None, None),
        P("section", "expert", None, None),
    )
    return jax.shard_map(
        body,
        mesh=mesh,
        in_specs=placed,
        out_specs=P("section", None, "expert", None),
        check_vma=False,
    )
```

profile of v0, /device:TPU:8, one launch (start us, length us, event | category | flops | bytes accessed | tf_op | source)
XLA Modules:
  0.0 645.4 jit_solution(5879649925889089358)
XLA Ops:
  0.9 643.8 %while.18 = (s32[]{:T(128)}, bf16[8,768]{1,0:T(8,128)(2,1)S(1)}, bf16[16,8,768]{2,1,0:T(8,128)(2,1)S(1)}, pred[]{:T(512)}, s32[]{:T(128)}, /*index=5*/bf16[16,8,...) while((s32[]{:T(128)}, bf16[8,768]{1,0:T(8,128)(2,1)S(1)}, ...), condition=%wide.region_6.7_spmd.clone, body=%wide.region_0.6_spmd.clone.sunk | while | flops 304748096 | bytes 10243028 | solution.py:111
  3.5 5.2 all_gather.12
  8.9 6.0 fusion.62
  31.5 5.2 all_gather.12
  36.9 6.0 fusion.62
  64.9 6.0 fusion.62
  87.5 5.2 all_gather.12
  92.9 6.0 fusion.62
  120.8 6.0 fusion.62
  148.8 6.0 fusion.62
  171.4 5.2 all_gather.12
  176.8 6.0 fusion.62
  204.8 6.0 fusion.62
  232.8 6.0 fusion.62
  255.4 5.2 all_gather.12
  260.8 6.0 fusion.62
  283.4 5.2 all_gather.12
  288.8 6.0 fusion.62
  316.8 6.0 fusion.62
  339.4 5.2 all_gather.12
  344.8 6.0 fusion.62
  367.4 5.2 all_gather.12
  372.8 6.0 fusion.62
  400.7 6.0 fusion.62
  428.7 6.0 fusion.62
  456.7 6.0 fusion.62
  484.7 6.0 fusion.62
  512.7 6.0 fusion.62
  540.7 6.0 fusion.62
  568.7 6.0 fusion.62
  596.7 6.0 fusion.62
  624.7 6.0 fusion.62
  (756 shorter events, 462.6 us)
Async XLA Ops:
  14.9 7.3 %all-to-all-start = ((bf16[4,8,768]{2,1,0:T(8,128)(2,1)}), bf16[4,8,768]{2,1,0:T(8,128)(2,1)S(1)}, u32[]{:S(2)}, u32[]{:S(2)}) async-start(bf16[4,8,768]{2,1,0:T(8,128)(2,1)} %fusion.62), calls=%async_computation | async-start | bytes 98304 | tf_op jit(solution)/shard_map/while/body/eval_jaxpr/all_to_all | solution.py:52
  22.5 6.5 %collective-permute-start = (bf16[8,768]{1,0:T(8,128)(2,1)S(1)}, bf16[8,768]{1,0:T(8,128)(2,1)S(1)}, u32[]{:S(2)}, u32[]{:S(2)}) collective-permute-start(bf16[8,768]{1,0:T(8,128)(2,1)S(1)} %get-tuple-element.505), channel_id=1, source_target_pairs={{0,4},{4,8},{8,12},{12,16},{16,20},{20,24},{24,28},{1,5},{5,9},{9,... | collective-permute-start | bytes 36872 | tf_op jit(solution)/shard_map/while/body/eval_jaxpr/ppermute | solution.py:12
  42.9 7.3 %all-to-all-start = ((bf16[4,8,768]{2,1,0:T(8,128)(2,1)}), bf16[4,8,768]{2,1,0:T(8,128)(2,1)S(1)}, u32[]{:S(2)}, u32[]{:S(2)}) async-start(bf16[4,8,768]{2,1,0:T(8,128)(2,1)} %fusion.62), calls=%async_computation | async-start | bytes 98304 | tf_op jit(solution)/shard_map/while/body/eval_jaxpr/all_to_all | solution.py:52
  50.5 6.5 %collective-permute-start = (bf16[8,768]{1,0:T(8,128)(2,1)S(1)}, bf16[8,768]{1,0:T(8,128)(2,1)S(1)}, u32[]{:S(2)}, u32[]{:S(2)}) collective-permute-start(bf16[8,768]{1,0:T(8,128)(2,1)S(1)} %get-tuple-element.505), channel_id=1, source_target_pairs={{0,4},{4,8},{8,12},{12,16},{16,20},{20,24},{24,28},{1,5},{5,9},{9,... | collective-permute-start | bytes 36872 | tf_op jit(solution)/shard_map/while/body/eval_jaxpr/ppermute | solution.py:12
  70.9 7.3 %all-to-all-start = ((bf16[4,8,768]{2,1,0:T(8,128)(2,1)}), bf16[4,8,768]{2,1,0:T(8,128)(2,1)S(1)}, u32[]{:S(2)}, u32[]{:S(2)}) async-start(bf16[4,8,768]{2,1,0:T(8,128)(2,1)} %fusion.62), calls=%async_computation | async-start | bytes 98304 | tf_op jit(solution)/shard_map/while/body/eval_jaxpr/all_to_all | solution.py:52
  78.5 6.5 %collective-permute-start = (bf16[8,768]{1,0:T(8,128)(2,1)S(1)}, bf16[8,768]{1,0:T(8,128)(2,1)S(1)}, u32[]{:S(2)}, u32[]{:S(2)}) collective-permute-start(bf16[8,768]{1,0:T(8,128)(2,1)S(1)} %get-tuple-element.505), channel_id=1, source_target_pairs={{0,4},{4,8},{8,12},{12,16},{16,20},{20,24},{24,28},{1,5},{5,9},{9,... | collective-permute-start | bytes 36872 | tf_op jit(solution)/shard_map/while/body/eval_jaxpr/ppermute | solution.py:12
  98.9 7.3 %all-to-all-start = ((bf16[4,8,768]{2,1,0:T(8,128)(2,1)}), bf16[4,8,768]{2,1,0:T(8,128)(2,1)S(1)}, u32[]{:S(2)}, u32[]{:S(2)}) async-start(bf16[4,8,768]{2,1,0:T(8,128)(2,1)} %fusion.62), calls=%async_computation | async-start | bytes 98304 | tf_op jit(solution)/shard_map/while/body/eval_jaxpr/all_to_all | solution.py:52
  106.5 6.5 %collective-permute-start = (bf16[8,768]{1,0:T(8,128)(2,1)S(1)}, bf16[8,768]{1,0:T(8,128)(2,1)S(1)}, u32[]{:S(2)}, u32[]{:S(2)}) collective-permute-start(bf16[8,768]{1,0:T(8,128)(2,1)S(1)} %get-tuple-element.505), channel_id=1, source_target_pairs={{0,4},{4,8},{8,12},{12,16},{16,20},{20,24},{24,28},{1,5},{5,9},{9,... | collective-permute-start | bytes 36872 | tf_op jit(solution)/shard_map/while/body/eval_jaxpr/ppermute | solution.py:12
  126.9 7.3 %all-to-all-start = ((bf16[4,8,768]{2,1,0:T(8,128)(2,1)}), bf16[4,8,768]{2,1,0:T(8,128)(2,1)S(1)}, u32[]{:S(2)}, u32[]{:S(2)}) async-start(bf16[4,8,768]{2,1,0:T(8,128)(2,1)} %fusion.62), calls=%async_computation | async-start | bytes 98304 | tf_op jit(solution)/shard_map/while/body/eval_jaxpr/all_to_all | solution.py:52
  134.4 6.5 %collective-permute-start = (bf16[8,768]{1,0:T(8,128)(2,1)S(1)}, bf16[8,768]{1,0:T(8,128)(2,1)S(1)}, u32[]{:S(2)}, u32[]{:S(2)}) collective-permute-start(bf16[8,768]{1,0:T(8,128)(2,1)S(1)} %get-tuple-element.505), channel_id=1, source_target_pairs={{0,4},{4,8},{8,12},{12,16},{16,20},{20,24},{24,28},{1,5},{5,9},{9,... | collective-permute-start | bytes 36872 | tf_op jit(solution)/shard_map/while/body/eval_jaxpr/ppermute | solution.py:12
  154.9 7.3 %all-to-all-start = ((bf16[4,8,768]{2,1,0:T(8,128)(2,1)}), bf16[4,8,768]{2,1,0:T(8,128)(2,1)S(1)}, u32[]{:S(2)}, u32[]{:S(2)}) async-start(bf16[4,8,768]{2,1,0:T(8,128)(2,1)} %fusion.62), calls=%async_computation | async-start | bytes 98304 | tf_op jit(solution)/shard_map/while/body/eval_jaxpr/all_to_all | solution.py:52
  162.4 6.5 %collective-permute-start = (bf16[8,768]{1,0:T(8,128)(2,1)S(1)}, bf16[8,768]{1,0:T(8,128)(2,1)S(1)}, u32[]{:S(2)}, u32[]{:S(2)}) collective-permute-start(bf16[8,768]{1,0:T(8,128)(2,1)S(1)} %get-tuple-element.505), channel_id=1, source_target_pairs={{0,4},{4,8},{8,12},{12,16},{16,20},{20,24},{24,28},{1,5},{5,9},{9,... | collective-permute-start | bytes 36872 | tf_op jit(solution)/shard_map/while/body/eval_jaxpr/ppermute | solution.py:12
  182.9 7.3 %all-to-all-start = ((bf16[4,8,768]{2,1,0:T(8,128)(2,1)}), bf16[4,8,768]{2,1,0:T(8,128)(2,1)S(1)}, u32[]{:S(2)}, u32[]{:S(2)}) async-start(bf16[4,8,768]{2,1,0:T(8,128)(2,1)} %fusion.62), calls=%async_computation | async-start | bytes 98304 | tf_op jit(solution)/shard_map/while/body/eval_jaxpr/all_to_all | solution.py:52
  190.4 6.5 %collective-permute-start = (bf16[8,768]{1,0:T(8,128)(2,1)S(1)}, bf16[8,768]{1,0:T(8,128)(2,1)S(1)}, u32[]{:S(2)}, u32[]{:S(2)}) collective-permute-start(bf16[8,768]{1,0:T(8,128)(2,1)S(1)} %get-tuple-element.505), channel_id=1, source_target_pairs={{0,4},{4,8},{8,12},{12,16},{16,20},{20,24},{24,28},{1,5},{5,9},{9,... | collective-permute-start | bytes 36872 | tf_op jit(solution)/shard_map/while/body/eval_jaxpr/ppermute | solution.py:12
  210.9 7.3 %all-to-all-start = ((bf16[4,8,768]{2,1,0:T(8,128)(2,1)}), bf16[4,8,768]{2,1,0:T(8,128)(2,1)S(1)}, u32[]{:S(2)}, u32[]{:S(2)}) async-start(bf16[4,8,768]{2,1,0:T(8,128)(2,1)} %fusion.62), calls=%async_computation | async-start | bytes 98304 | tf_op jit(solution)/shard_map/while/body/eval_jaxpr/all_to_all | solution.py:52
  238.8 7.3 %all-to-all-start = ((bf16[4,8,768]{2,1,0:T(8,128)(2,1)}), bf16[4,8,768]{2,1,0:T(8,128)(2,1)S(1)}, u32[]{:S(2)}, u32[]{:S(2)}) async-start(bf16[4,8,768]{2,1,0:T(8,128)(2,1)} %fusion.62), calls=%async_computation | async-start | bytes 98304 | tf_op jit(solution)/shard_map/while/body/eval_jaxpr/all_to_all | solution.py:52
  246.4 6.5 %collective-permute-start = (bf16[8,768]{1,0:T(8,128)(2,1)S(1)}, bf16[8,768]{1,0:T(8,128)(2,1)S(1)}, u32[]{:S(2)}, u32[]{:S(2)}) collective-permute-start(bf16[8,768]{1,0:T(8,128)(2,1)S(1)} %get-tuple-element.505), channel_id=1, source_target_pairs={{0,4},{4,8},{8,12},{12,16},{16,20},{20,24},{24,28},{1,5},{5,9},{9,... | collective-permute-start | bytes 36872 | tf_op jit(solution)/shard_map/while/body/eval_jaxpr/ppermute | solution.py:12
  266.8 7.3 %all-to-all-start = ((bf16[4,8,768]{2,1,0:T(8,128)(2,1)}), bf16[4,8,768]{2,1,0:T(8,128)(2,1)S(1)}, u32[]{:S(2)}, u32[]{:S(2)}) async-start(bf16[4,8,768]{2,1,0:T(8,128)(2,1)} %fusion.62), calls=%async_computation | async-start | bytes 98304 | tf_op jit(solution)/shard_map/while/body/eval_jaxpr/all_to_all | solution.py:52
  294.8 7.3 %all-to-all-start = ((bf16[4,8,768]{2,1,0:T(8,128)(2,1)}), bf16[4,8,768]{2,1,0:T(8,128)(2,1)S(1)}, u32[]{:S(2)}, u32[]{:S(2)}) async-start(bf16[4,8,768]{2,1,0:T(8,128)(2,1)} %fusion.62), calls=%async_computation | async-start | bytes 98304 | tf_op jit(solution)/shard_map/while/body/eval_jaxpr/all_to_all | solution.py:52
  322.8 7.3 %all-to-all-start = ((bf16[4,8,768]{2,1,0:T(8,128)(2,1)}), bf16[4,8,768]{2,1,0:T(8,128)(2,1)S(1)}, u32[]{:S(2)}, u32[]{:S(2)}) async-start(bf16[4,8,768]{2,1,0:T(8,128)(2,1)} %fusion.62), calls=%async_computation | async-start | bytes 98304 | tf_op jit(solution)/shard_map/while/body/eval_jaxpr/all_to_all | solution.py:52
  330.4 6.5 %collective-permute-start = (bf16[8,768]{1,0:T(8,128)(2,1)S(1)}, bf16[8,768]{1,0:T(8,128)(2,1)S(1)}, u32[]{:S(2)}, u32[]{:S(2)}) collective-permute-start(bf16[8,768]{1,0:T(8,128)(2,1)S(1)} %get-tuple-element.505), channel_id=1, source_target_pairs={{0,4},{4,8},{8,12},{12,16},{16,20},{20,24},{24,28},{1,5},{5,9},{9,... | collective-permute-start | bytes 36872 | tf_op jit(solution)/shard_map/while/body/eval_jaxpr/ppermute | solution.py:12
  350.8 7.3 %all-to-all-start = ((bf16[4,8,768]{2,1,0:T(8,128)(2,1)}), bf16[4,8,768]{2,1,0:T(8,128)(2,1)S(1)}, u32[]{:S(2)}, u32[]{:S(2)}) async-start(bf16[4,8,768]{2,1,0:T(8,128)(2,1)} %fusion.62), calls=%async_computation | async-start | bytes 98304 | tf_op jit(solution)/shard_map/while/body/eval_jaxpr/all_to_all | solution.py:52
  378.8 7.3 %all-to-all-start = ((bf16[4,8,768]{2,1,0:T(8,128)(2,1)}), bf16[4,8,768]{2,1,0:T(8,128)(2,1)S(1)}, u32[]{:S(2)}, u32[]{:S(2)}) async-start(bf16[4,8,768]{2,1,0:T(8,128)(2,1)} %fusion.62), calls=%async_computation | async-start | bytes 98304 | tf_op jit(solution)/shard_map/while/body/eval_jaxpr/all_to_all | solution.py:52
  406.8 7.3 %all-to-all-start = ((bf16[4,8,768]{2,1,0:T(8,128)(2,1)}), bf16[4,8,768]{2,1,0:T(8,128)(2,1)S(1)}, u32[]{:S(2)}, u32[]{:S(2)}) async-start(bf16[4,8,768]{2,1,0:T(8,128)(2,1)} %fusion.62), calls=%async_computation | async-start | bytes 98304 | tf_op jit(solution)/shard_map/while/body/eval_jaxpr/all_to_all | solution.py:52
  434.8 7.3 %all-to-all-start = ((bf16[4,8,768]{2,1,0:T(8,128)(2,1)}), bf16[4,8,768]{2,1,0:T(8,128)(2,1)S(1)}, u32[]{:S(2)}, u32[]{:S(2)}) async-start(bf16[4,8,768]{2,1,0:T(8,128)(2,1)} %fusion.62), calls=%async_computation | async-start | bytes 98304 | tf_op jit(solution)/shard_map/while/body/eval_jaxpr/all_to_all | solution.py:52
  462.8 7.3 %all-to-all-start = ((bf16[4,8,768]{2,1,0:T(8,128)(2,1)}), bf16[4,8,768]{2,1,0:T(8,128)(2,1)S(1)}, u32[]{:S(2)}, u32[]{:S(2)}) async-start(bf16[4,8,768]{2,1,0:T(8,128)(2,1)} %fusion.62), calls=%async_computation | async-start | bytes 98304 | tf_op jit(solution)/shard_map/while/body/eval_jaxpr/all_to_all | solution.py:52
  490.8 7.3 %all-to-all-start = ((bf16[4,8,768]{2,1,0:T(8,128)(2,1)}), bf16[4,8,768]{2,1,0:T(8,128)(2,1)S(1)}, u32[]{:S(2)}, u32[]{:S(2)}) async-start(bf16[4,8,768]{2,1,0:T(8,128)(2,1)} %fusion.62), calls=%async_computation | async-start | bytes 98304 | tf_op jit(solution)/shard_map/while/body/eval_jaxpr/all_to_all | solution.py:52
  518.7 7.3 %all-to-all-start = ((bf16[4,8,768]{2,1,0:T(8,128)(2,1)}), bf16[4,8,768]{2,1,0:T(8,128)(2,1)S(1)}, u32[]{:S(2)}, u32[]{:S(2)}) async-start(bf16[4,8,768]{2,1,0:T(8,128)(2,1)} %fusion.62), calls=%async_computation | async-start | bytes 98304 | tf_op jit(solution)/shard_map/while/body/eval_jaxpr/all_to_all | solution.py:52
  546.7 7.3 %all-to-all-start = ((bf16[4,8,768]{2,1,0:T(8,128)(2,1)}), bf16[4,8,768]{2,1,0:T(8,128)(2,1)S(1)}, u32[]{:S(2)}, u32[]{:S(2)}) async-start(bf16[4,8,768]{2,1,0:T(8,128)(2,1)} %fusion.62), calls=%async_computation | async-start | bytes 98304 | tf_op jit(solution)/shard_map/while/body/eval_jaxpr/all_to_all | solution.py:52
  574.7 7.3 %all-to-all-start = ((bf16[4,8,768]{2,1,0:T(8,128)(2,1)}), bf16[4,8,768]{2,1,0:T(8,128)(2,1)S(1)}, u32[]{:S(2)}, u32[]{:S(2)}) async-start(bf16[4,8,768]{2,1,0:T(8,128)(2,1)} %fusion.62), calls=%async_computation | async-start | bytes 98304 | tf_op jit(solution)/shard_map/while/body/eval_jaxpr/all_to_all | solution.py:52
  602.7 7.3 %all-to-all-start = ((bf16[4,8,768]{2,1,0:T(8,128)(2,1)}), bf16[4,8,768]{2,1,0:T(8,128)(2,1)S(1)}, u32[]{:S(2)}, u32[]{:S(2)}) async-start(bf16[4,8,768]{2,1,0:T(8,128)(2,1)} %fusion.62), calls=%async_computation | async-start | bytes 98304 | tf_op jit(solution)/shard_map/while/body/eval_jaxpr/all_to_all | solution.py:52
  630.7 7.3 %all-to-all-start = ((bf16[4,8,768]{2,1,0:T(8,128)(2,1)}), bf16[4,8,768]{2,1,0:T(8,128)(2,1)S(1)}, u32[]{:S(2)}, u32[]{:S(2)}) async-start(bf16[4,8,768]{2,1,0:T(8,128)(2,1)} %fusion.62), calls=%async_computation | async-start | bytes 98304 | tf_op jit(solution)/shard_map/while/body/eval_jaxpr/all_to_all | solution.py:52
  (38 other events, 306.1 us)
where the time goes:
time: 651 us; the launch traced here: 645 us
  waiting for transfers between devices  190 us (29%)
  matrix products  150 us (23%)
  starting transfers between devices  121 us (19%)
  blocking collectives  120 us (18%)
  other arithmetic  51.5 us (8%)
  local copies, waits for them, and re-layouts  10.7 us (2%)
    dot_general x23, matrix products, apply_expert(): jnp.dot(hidden, expert_out, preferred_element_type=jnp.float32)  139 us
    all_gather x23, blocking collectives, apply_layer(): lax.all_gather(normed, 'expert', axis=0, tiled=True)  120 us
    ppermute x23, waiting for transfers between devices, from_behind(): return lax.ppermute(block, axis, route)  103 us
    all_to_all x23, waiting for transfers between devices, apply_expert(): lax.all_to_all(produced.reshape(received.shape), 'expert', split_axis=0,...  87.2 us
    all_to_all x23, starting transfers between devices, apply_expert(): lax.all_to_all(produced.reshape(received.shape), 'expert', split_axis=0,...  75.3 us
    ppermute x23, starting transfers between devices, from_behind(): return lax.ppermute(block, axis, route)  46 us
    reduce_sum x23, other arithmetic, apply_layer(): jnp.mean(stream * stream, axis=-1, keepdims=True) + epsilon  19.2 us
    mul x23, other arithmetic, apply_layer(): normed = (stream * inverse * gain_row).astype(jnp.bfloat16)  16.1 us
  transfers between devices with their start and end apart: 46, of which 46 were waited for; matrix products, arithmetic and copies ran while one was open for 1% of the time, Pallas kernels for 0%

commit v1 on v0

v1 whole, which is shorter than its diff:
```python
import functools

import jax
import jax.numpy as jnp
from jax import lax
from jax.experimental import pallas as pl
from jax.experimental.pallas import tpu as pltpu
from jax.sharding import PartitionSpec as P

epsilon = 1e-06
CHUNKS = 2
LANES = 128
UNROLLED = 32


def expert_kernel(
    tile, mine_ref, other_ref, mask_ref, gain_ref, router_ref, in_ref, out_ref,
    send_ref, keep_ref, in_tiles, out_tiles, normed, gate, total, sems,
):
    steps = in_tiles.shape[0]
    half = mine_ref.shape[0]
    block = min(2 * half, 256)

    def copies(i):
        start = pl.multiple_of(i * tile, tile)
        return (
            pltpu.make_async_copy(in_ref.at[:, pl.ds(start, tile)], in_tiles.at[i], sems.at[0, i]),
            pltpu.make_async_copy(out_ref.at[pl.ds(start, tile), :], out_tiles.at[i], sems.at[1, i]),
        )

    for i in range(steps):
        for copy in copies(i):
            copy.start()
    for place, ref in ((0, mine_ref), (half, other_ref)):

        def normalize(g, carry):
            source = pl.ds(pl.multiple_of(g * (block // 2), block // 2), block // 2)
            stream = ref[source, :].astype(jnp.float32)
            inverse = lax.rsqrt(jnp.mean(stream * stream, axis=-1, keepdims=True) + epsilon)
            value = (stream * inverse * gain_ref[...]).astype(jnp.bfloat16)
            rows = pl.ds(pl.multiple_of(place + g * (block // 2), block // 2), block // 2)
            normed[rows, :] = value
            logits = jnp.dot(value, router_ref[...], preferred_element_type=jnp.float32)
            gate[rows, :] = jax.nn.sigmoid(logits) * mask_ref[rows, :]
            total[rows, :] = jnp.zeros((block // 2, total.shape[1]), jnp.float32)
            return carry

        lax.fori_loop(0, 2 * half // block, normalize, 0)

    def step(i, carry):
        for copy in copies(i):
            copy.wait()

        def group(g, carry):
            rows = pl.ds(pl.multiple_of(g * block, block), block)
            hidden = jnp.dot(normed[rows, :], in_tiles[i], preferred_element_type=jnp.float32)
            hidden = jnp.maximum(hidden, 0.0).astype(jnp.bfloat16)
            total[rows, :] += jnp.dot(hidden, out_tiles[i], preferred_element_type=jnp.float32)
            return carry

        return lax.fori_loop(0, 2 * half // block, group, carry)

    lax.fori_loop(0, steps, step, 0)
    for place, ref in ((0, send_ref), (half, keep_ref)):

        def finish(g, carry):
            rows = pl.ds(pl.multiple_of(place + g * (block // 2), block // 2), block // 2)
            target = pl.ds(pl.multiple_of(g * (block // 2), block // 2), block // 2)
            for column in range(0, total.shape[1], LANES):
                lanes = pl.ds(column, LANES)
                ref[target, lanes] = (total[rows, lanes] * gate[rows, :]).astype(ref.dtype)
            return carry

        lax.fori_loop(0, 2 * half // block, finish, 0)


def run_expert(mine, other, mask, gain, router, weight_in, weight_out):
    half, features = mine.shape
    hidden_total = weight_in.shape[1]
    tile = 512
    steps = hidden_total // tile
    rows = 2 * half
    vmem, anywhere = pltpu.VMEM, pl.ANY
    return pl.pallas_call(
        functools.partial(expert_kernel, tile),
        out_shape=(jax.ShapeDtypeStruct(mine.shape, jnp.bfloat16),) * 2,
        in_specs=[pl.BlockSpec(memory_space=vmem)] * 5 + [pl.BlockSpec(memory_space=anywhere)] * 2,
        out_specs=(pl.BlockSpec(memory_space=vmem),) * 2,
        scratch_shapes=[
            pltpu.VMEM((steps, features, tile), jnp.bfloat16),
            pltpu.VMEM((steps, tile, features), jnp.bfloat16),
            pltpu.VMEM((rows, features), jnp.bfloat16),
            pltpu.VMEM((rows, LANES), jnp.float32),
            pltpu.VMEM((rows, features), jnp.float32),
            pltpu.SemaphoreType.DMA((2, steps)),
        ],
        compiler_params=pltpu.CompilerParams(vmem_limit_bytes=40 * 2**20),
        cost_estimate=pl.CostEstimate(
            flops=4 * rows * features * hidden_total,
            bytes_accessed=4 * features * hidden_total,
            transcendentals=0,
        ),
    )(mine, other, mask, gain, router, weight_in, weight_out)


def body(tokens, route_ids, router, norm_gain, weight_in, weight_out):
    sections, experts = lax.axis_size("section"), lax.axis_size("expert")
    section, member = lax.axis_index("section"), lax.axis_index("expert")
    chip, core = member // 2, member % 2
    chips = experts // 2
    micro_count, tok_rows, features = tokens.shape
    part = micro_count // CHUNKS
    rows = part * tok_rows
    gain = norm_gain.astype(jnp.float32)
    expert_in, expert_out = weight_in[0, 0], weight_out[0, 0]
    column = lax.dynamic_slice_in_dim(router[0], member, 1, axis=1)
    column = jnp.broadcast_to(column, (features, LANES))

    named = jnp.any(route_ids[0] == member, axis=-1).reshape(CHUNKS, part, chips, 2, tok_rows)
    named = named.transpose(0, 3, 2, 1, 4)
    named = jnp.where(core == 0, named[:, ::-1], named).astype(jnp.float32)
    masks = jnp.broadcast_to(named.reshape(CHUNKS, -1, 1), (CHUNKS, experts * rows, LANES))

    def place(s, e):
        return s * experts + e

    def across(value, other_of):
        pairs = [
            (place(s, e), place(*other_of(s, e))) for s in range(sections) for e in range(experts)
        ]
        return lax.ppermute(value, ("section", "expert"), pairs)

    def paired(s, odd):
        other = s - 1 if (s % 2 == 0) == odd else s + 1
        return other if 0 <= other < sections else s

    def to_paired(value, odd, flip):
        def other_of(s, e):
            other = paired(s, odd)
            return (other, e ^ (flip if other != s else (flip or 1)))

        return across(value, other_of)

    def swapped(value):
        return across(value, lambda s, e: (s, e ^ 1))

    def own_of(other):
        return lax.dynamic_slice_in_dim(other, chip * rows, rows, axis=0)

    mine, others = [], []
    for j in range(CHUNKS):
        entering = lax.all_gather(tokens[j * part : (j + 1) * part].reshape(rows, features), "expert")
        entering = entering.reshape(chips, 2, rows, features)
        mine.append(lax.dynamic_index_in_dim(entering, 1 - core, 1, False).reshape(-1, features))
        others.append(lax.dynamic_index_in_dim(entering, core, 1, False).reshape(-1, features))
    saved = [jnp.zeros((rows, features), jnp.bfloat16) for _ in range(CHUNKS)]

    def turn_of(turn, odd, state):
        mine, others, saved = (list(part_state) for part_state in state)
        for j in range(CHUNKS):
            saved[j] = jnp.where(section == turn, own_of(others[j]), saved[j])
            send, keep = run_expert(
                mine[j], others[j], masks[j], gain, column, expert_in, expert_out
            )
            stream = jnp.where(chip == 0, others[j], jnp.zeros_like(others[j]))
            partial = keep.astype(jnp.float32) + swapped(send).astype(jnp.float32)
            partial = (partial + stream.astype(jnp.float32)).astype(jnp.bfloat16)
            arrived = [to_paired(partial, odd, 2 * k + 1) for k in range(chips)]
            mine[j] = sum(a.astype(jnp.float32) for a in arrived).astype(jnp.bfloat16)
            others[j] = swapped(mine[j])
        return mine, others, saved

    def two_turns(pair, state):
        return turn_of(2 * pair + 1, True, turn_of(2 * pair, False, state))

    state = (mine, others, saved)
    if sections * chips <= UNROLLED:
        for pair in range(sections // 2):
            state = two_turns(pair, state)
    else:
        state = lax.fori_loop(0, sections // 2, two_turns, state)
    mine, others, saved = state
    whole = jnp.concatenate(saved, axis=0)
    from_even, from_odd = to_paired(whole, False, 0), to_paired(whole, True, 0)
    returned = jnp.where(section % 2 == 0, from_even, from_odd)
    last = jnp.concatenate([own_of(other) for other in others], axis=0)
    states = jnp.where(section == sections - 1, last, returned)
    return states.reshape(1, micro_count, tok_rows, features)


def solution(mesh):
    placed = (
        P(None, "expert", None),
        P("section", None, None, None),
        P("section", None, None),
        P("section", None),
        P("section", "expert", None, None),
        P("section", "expert", None, None),
    )
    return jax.shard_map(
        body,
        mesh=mesh,
        in_specs=placed,
        out_specs=P("section", None, "expert", None),
        check_vma=False,
    )
```

time: 651 us -> 313 us (0.48)
  matrix products: 150 us -> 0 us
  blocking collectives: 120 us -> 13 us
  Pallas kernels: 0 us -> 92.1 us
  waiting for transfers between devices: 190 us -> 123 us
  starting transfers between devices: 121 us -> 58.8 us
  other arithmetic: 51.5 us -> 4 us
  local copies, waits for them, and re-layouts: 10.7 us -> 21.2 us
    dot_general x92 -> x0, matrix products: 150 us -> none  [the longest x23 139 us: apply_expert(): jnp.dot(hidden, expert_out, preferred_element_type=jnp.float32)]
    all_gather x23 -> x2, blocking collectives: 120 us -> 13 us  [body(): lax.all_gather(tokens[j * part:(j + 1) * part].reshape(rows, features), '...]
    pallas_call x0 -> x16, Pallas kernels: none -> 92.1 us  [run_expert(): pl.pallas_call(functools.partial(expert_kernel, tile), out_shape=(jax.Sha...]
    all_to_all x23 -> x0, waiting for transfers between devices: 87.2 us -> none  [apply_expert(): lax.all_to_all(produced.reshape(received.shape), 'expert', split_axis=0,...]
    all_to_all x23 -> x0, starting transfers between devices: 75.3 us -> none  [apply_expert(): lax.all_to_all(produced.reshape(received.shape), 'expert', split_axis=0,...]
    reduce_sum x92 -> x0, other arithmetic: 26.7 us -> none  [the longest x23 19.2 us: apply_layer(): jnp.mean(stream * stream, axis=-1, keepdims=True) + epsilon]
    ppermute x23 -> x66, waiting for transfers between devices: 103 us -> 123 us  [across(): return lax.ppermute(value, ('section', 'expert'), pairs)]
    unnamed x3 -> x26, local copies, waits for them, and re-layouts: 1.56 us -> 19.4 us
  transfers between devices with their start and end apart: 46 -> 66, of which waited for: 46 -> 33; matrix products, arithmetic and copies ran while one was open for 1% -> 1% of each run, Pallas kernels for 0% -> 28%
where the time goes in v1:
time: 313 us; the launch traced here: 312 us
  waiting for transfers between devices  123 us (39%)
  Pallas kernels  92.1 us (29%)
  starting transfers between devices  58.8 us (19%)
  local copies, waits for them, and re-layouts  21.2 us (7%)
  blocking collectives  13 us (4%)
  other arithmetic  4 us (1%)
    ppermute x66, waiting for transfers between devices, across(): return lax.ppermute(value, ('section', 'expert'), pairs)  123 us
    pallas_call x16, Pallas kernels, run_expert(): pl.pallas_call(functools.partial(expert_kernel, tile), out_shape=(jax.Sha...  92.1 us
    ppermute x66, starting transfers between devices, across(): return lax.ppermute(value, ('section', 'expert'), pairs)  58.8 us
    unnamed x26, local copies, waits for them, and re-layouts  19.4 us
    all_gather x2, blocking collectives, body(): lax.all_gather(tokens[j * part:(j + 1) * part].reshape(rows, features), '...  13 us
  transfers between devices with their start and end apart: 66, of which 33 were waited for; matrix products, arithmetic and copies ran while one was open for 1% of the time, Pallas kernels for 28%

profile of v1, /device:TPU:8, one launch (start us, length us, event | category | flops | bytes accessed | tf_op | source)
XLA Modules:
  0.0 312.3 jit_solution(5338613091057676449)
XLA Ops:
  1.0 6.5 %all_gather.6 = bf16[4,64,768]{2,1,0:T(8,128)(2,1)S(1)} all-gather(bf16[1,64,768]{2,1,0:T(8,128)(2,1)S(1)} %get-tuple-element.73), channel_id=1, replica_groups=mesh['section'=8,'expert'=4] {'expert'}, dimensions={0}, use_global_device_ids=true | all-gather | bytes 491520 | tf_op jit(solution)/shard_map/all_gather | solution.py:152
  7.5 6.6 %all_gather.7 = bf16[4,64,768]{2,1,0:T(8,128)(2,1)S(1)} all-gather(bf16[1,64,768]{2,1,0:T(8,128)(2,1)S(1)} %get-tuple-element.74), channel_id=1, replica_groups=mesh['section'=8,'expert'=4] {'expert'}, dimensions={0}, use_global_device_ids=true | all-gather | bytes 491520 | tf_op jit(solution)/shard_map/all_gather | solution.py:152
  20.9 5.7 %shard_map.64 = (bf16[128,768]{1,0:T(8,128)(2,1)S(1)}, bf16[128,768]{1,0:T(8,128)(2,1)S(1)}) custom-call(bf16[128,768]{1,0:T(8,128)(2,1)S(1)} %bitcast.59, bf16[128,768]{1,0:T(8,128)(2,1)S(1)} %bitcast.56, f32[256,128]{1,0:T(8,128)S(1)} %broadcast_in_dim.19.mask_ref, f32[1,768]{1,0:T(1,128)S(1)} %copy-done.11, ...), custom_call_target="tpu_custom_call" | custom-call | flops 2415919104 | bytes 9437184 | tf_op jit(solution)/shard_map/pallas_call | solution.py:84
  31.9 5.7 %shard_map.72 = (bf16[128,768]{1,0:T(8,128)(2,1)S(1)}, bf16[128,768]{1,0:T(8,128)(2,1)S(1)}) custom-call(bf16[128,768]{1,0:T(8,128)(2,1)S(1)} %bitcast.58, bf16[128,768]{1,0:T(8,128)(2,1)S(1)} %bitcast.54, f32[256,128]{1,0:T(8,128)S(1)} %broadcast_in_dim.23.mask_ref, f32[1,768]{1,0:T(1,128)S(1)} %copy-done.12, ...), custom_call_target="tpu_custom_call" | custom-call | flops 2415919104 | bytes 9437184 | tf_op jit(solution)/shard_map/pallas_call | solution.py:84
  44.8 4.7 %collective-permute-done.2 = bf16[128,768]{1,0:T(8,128)(2,1)S(1)} collective-permute-done((bf16[128,768]{1,0:T(8,128)(2,1)S(1)}, bf16[128,768]{1,0:T(8,128)(2,1)S(1)}, u32[]{:S(2)}, u32[]{:S(2)}) %collective-permute-start.2) | collective-permute-done | bytes 196640 | tf_op jit(solution)/shard_map/ppermute | solution.py:131
  53.2 4.7 %collective-permute-done.34 = bf16[128,768]{1,0:T(8,128)(2,1)S(1)} collective-permute-done((bf16[128,768]{1,0:T(8,128)(2,1)S(1)}, bf16[128,768]{1,0:T(8,128)(2,1)S(1)}, u32[]{:S(2)}, u32[]{:S(2)}) %collective-permute-start.34) | collective-permute-done | bytes 196640 | tf_op jit(solution)/shard_map/ppermute | solution.py:131
  63.1 5.7 %shard_map.65 = (bf16[128,768]{1,0:T(8,128)(2,1)S(1)}, bf16[128,768]{1,0:T(8,128)(2,1)S(1)}) custom-call(bf16[128,768]{1,0:T(8,128)(2,1)S(1)} %add_convert_fusion.30.mine_ref, bf16[128,768]{1,0:T(8,128)(2,1)S(1)} %collective-permute-done.3.other_ref, f32[256,128]{1,0:T(8,128)S(1)} %broadcast_in_dim.19.mask_ref, f32[1,768]{1,0:T(1,128)S(1)} %copy-done.12, ...), custom_call_target="tpu_custom_call" | custom-call | flops 2415919104 | bytes 9437184 | tf_op jit(solution)/shard_map/pallas_call | solution.py:84
  73.7 5.7 %shard_map.73 = (bf16[128,768]{1,0:T(8,128)(2,1)S(1)}, bf16[128,768]{1,0:T(8,128)(2,1)S(1)}) custom-call(bf16[128,768]{1,0:T(8,128)(2,1)S(1)} %add_convert_fusion.14.mine_ref, bf16[128,768]{1,0:T(8,128)(2,1)S(1)} %collective-permute-done.35.other_ref, f32[256,128]{1,0:T(8,128)S(1)} %broadcast_in_dim.23.mask_ref, f32[1,768]{1,0:T(1,128)S(1)} %copy-done.12, ...), custom_call_target="tpu_custom_call" | custom-call | flops 2415919104 | bytes 9437184 | tf_op jit(solution)/shard_map/pallas_call | solution.py:84
  87.8 4.5 %collective-permute-done.6 = bf16[128,768]{1,0:T(8,128)(2,1)S(1)} collective-permute-done((bf16[128,768]{1,0:T(8,128)(2,1)S(1)}, bf16[128,768]{1,0:T(8,128)(2,1)S(1)}, u32[]{:S(2)}, u32[]{:S(2)}) %collective-permute-start.6) | collective-permute-done | bytes 196640 | tf_op jit(solution)/shard_map/ppermute | solution.py:131
  96.3 4.5 %collective-permute-done.38 = bf16[128,768]{1,0:T(8,128)(2,1)S(1)} collective-permute-done((bf16[128,768]{1,0:T(8,128)(2,1)S(1)}, bf16[128,768]{1,0:T(8,128)(2,1)S(1)}, u32[]{:S(2)}, u32[]{:S(2)}) %collective-permute-start.38) | collective-permute-done | bytes 196640 | tf_op jit(solution)/shard_map/ppermute | solution.py:131
  101.0 5.7 %shard_map.66 = (bf16[128,768]{1,0:T(8,128)(2,1)S(1)}, bf16[128,768]{1,0:T(8,128)(2,1)S(1)}) custom-call(bf16[128,768]{1,0:T(8,128)(2,1)S(1)} %add_convert_fusion.28.mine_ref, bf16[128,768]{1,0:T(8,128)(2,1)S(1)} %collective-permute-done.7.other_ref, f32[256,128]{1,0:T(8,128)S(1)} %broadcast_in_dim.19.mask_ref, f32[1,768]{1,0:T(1,128)S(1)} %copy-done.12, ...), custom_call_target="tpu_custom_call" | custom-call | flops 2415919104 | bytes 9437184 | tf_op jit(solution)/shard_map/pallas_call | solution.py:84
  107.2 5.7 %shard_map.74 = (bf16[128,768]{1,0:T(8,128)(2,1)S(1)}, bf16[128,768]{1,0:T(8,128)(2,1)S(1)}) custom-call(bf16[128,768]{1,0:T(8,128)(2,1)S(1)} %add_convert_fusion.12.mine_ref, bf16[128,768]{1,0:T(8,128)(2,1)S(1)} %collective-permute-done.39.other_ref, f32[256,128]{1,0:T(8,128)S(1)} %broadcast_in_dim.23.mask_ref, f32[1,768]{1,0:T(1,128)S(1)} %copy-done.12, ...), custom_call_target="tpu_custom_call" | custom-call | flops 2415919104 | bytes 9437184 | tf_op jit(solution)/shard_map/pallas_call | solution.py:84
  129.1 4.4 %collective-permute-done.42 = bf16[128,768]{1,0:T(8,128)(2,1)S(1)} collective-permute-done((bf16[128,768]{1,0:T(8,128)(2,1)S(1)}, bf16[128,768]{1,0:T(8,128)(2,1)S(1)}, u32[]{:S(2)}, u32[]{:S(2)}) %collective-permute-start.42) | collective-permute-done | bytes 196640 | tf_op jit(solution)/shard_map/ppermute | solution.py:131
  134.0 5.9 %shard_map.67 = (bf16[128,768]{1,0:T(8,128)(2,1)S(1)}, bf16[128,768]{1,0:T(8,128)(2,1)S(1)}) custom-call(bf16[128,768]{1,0:T(8,128)(2,1)S(1)} %add_convert_fusion.26.mine_ref, bf16[128,768]{1,0:T(8,128)(2,1)S(1)} %collective-permute-done.11.other_ref, f32[256,128]{1,0:T(8,128)S(1)} %broadcast_in_dim.19.mask_ref, f32[1,768]{1,0:T(1,128)S(1)} %copy-done.12, ...), custom_call_target="tpu_custom_call" | custom-call | flops 2415919104 | bytes 9437184 | tf_op jit(solution)/shard_map/pallas_call | solution.py:84
  140.1 5.7 %shard_map.75 = (bf16[128,768]{1,0:T(8,128)(2,1)S(1)}, bf16[128,768]{1,0:T(8,128)(2,1)S(1)}) custom-call(bf16[128,768]{1,0:T(8,128)(2,1)S(1)} %add_convert_fusion.10.mine_ref, bf16[128,768]{1,0:T(8,128)(2,1)S(1)} %collective-permute-done.43.other_ref, f32[256,128]{1,0:T(8,128)S(1)} %broadcast_in_dim.23.mask_ref, f32[1,768]{1,0:T(1,128)S(1)} %copy-done.12, ...), custom_call_target="tpu_custom_call" | custom-call | flops 2415919104 | bytes 9437184 | tf_op jit(solution)/shard_map/pallas_call | solution.py:84
  154.2 4.8 %collective-permute-done.14 = bf16[128,768]{1,0:T(8,128)(2,1)S(1)} collective-permute-done((bf16[128,768]{1,0:T(8,128)(2,1)S(1)}, bf16[128,768]{1,0:T(8,128)(2,1)S(1)}, u32[]{:S(2)}, u32[]{:S(2)}) %collective-permute-start.14) | collective-permute-done | bytes 196640 | tf_op jit(solution)/shard_map/ppermute | solution.py:131
  162.7 4.8 %collective-permute-done.46 = bf16[128,768]{1,0:T(8,128)(2,1)S(1)} collective-permute-done((bf16[128,768]{1,0:T(8,128)(2,1)S(1)}, bf16[128,768]{1,0:T(8,128)(2,1)S(1)}, u32[]{:S(2)}, u32[]{:S(2)}) %collective-permute-start.46) | collective-permute-done | bytes 196640 | tf_op jit(solution)/shard_map/ppermute | solution.py:131
  167.8 5.7 %shard_map.68 = (bf16[128,768]{1,0:T(8,128)(2,1)S(1)}, bf16[128,768]{1,0:T(8,128)(2,1)S(1)}) custom-call(bf16[128,768]{1,0:T(8,128)(2,1)S(1)} %add_convert_fusion.24.mine_ref, bf16[128,768]{1,0:T(8,128)(2,1)S(1)} %collective-permute-done.15.other_ref, f32[256,128]{1,0:T(8,128)S(1)} %broadcast_in_dim.19.mask_ref, f32[1,768]{1,0:T(1,128)S(1)} %copy-done.12, ...), custom_call_target="tpu_custom_call" | custom-call | flops 2415919104 | bytes 9437184 | tf_op jit(solution)/shard_map/pallas_call | solution.py:84
  173.9 5.7 %shard_map.76 = (bf16[128,768]{1,0:T(8,128)(2,1)S(1)}, bf16[128,768]{1,0:T(8,128)(2,1)S(1)}) custom-call(bf16[128,768]{1,0:T(8,128)(2,1)S(1)} %add_convert_fusion.8.mine_ref, bf16[128,768]{1,0:T(8,128)(2,1)S(1)} %collective-permute-done.47.other_ref, f32[256,128]{1,0:T(8,128)S(1)} %broadcast_in_dim.23.mask_ref, f32[1,768]{1,0:T(1,128)S(1)} %copy-done.12, ...), custom_call_target="tpu_custom_call" | custom-call | flops 2415919104 | bytes 9437184 | tf_op jit(solution)/shard_map/pallas_call | solution.py:84
  200.1 5.7 %shard_map.69 = (bf16[128,768]{1,0:T(8,128)(2,1)S(1)}, bf16[128,768]{1,0:T(8,128)(2,1)S(1)}) custom-call(bf16[128,768]{1,0:T(8,128)(2,1)S(1)} %add_convert_fusion.22.mine_ref, bf16[128,768]{1,0:T(8,128)(2,1)S(1)} %collective-permute-done.19.other_ref, f32[256,128]{1,0:T(8,128)S(1)} %broadcast_in_dim.19.mask_ref, f32[1,768]{1,0:T(1,128)S(1)} %copy-done.12, ...), custom_call_target="tpu_custom_call" | custom-call | flops 2415919104 | bytes 9437184 | tf_op jit(solution)/shard_map/pallas_call | solution.py:84
  206.1 5.7 %shard_map.77 = (bf16[128,768]{1,0:T(8,128)(2,1)S(1)}, bf16[128,768]{1,0:T(8,128)(2,1)S(1)}) custom-call(bf16[128,768]{1,0:T(8,128)(2,1)S(1)} %add_convert_fusion.6.mine_ref, bf16[128,768]{1,0:T(8,128)(2,1)S(1)} %collective-permute-done.51.other_ref, f32[256,128]{1,0:T(8,128)S(1)} %broadcast_in_dim.23.mask_ref, f32[1,768]{1,0:T(1,128)S(1)} %copy-done.12, ...), custom_call_target="tpu_custom_call" | custom-call | flops 2415919104 | bytes 9437184 | tf_op jit(solution)/shard_map/pallas_call | solution.py:84
  220.2 4.8 %collective-permute-done.22 = bf16[128,768]{1,0:T(8,128)(2,1)S(1)} collective-permute-done((bf16[128,768]{1,0:T(8,128)(2,1)S(1)}, bf16[128,768]{1,0:T(8,128)(2,1)S(1)}, u32[]{:S(2)}, u32[]{:S(2)}) %collective-permute-start.22) | collective-permute-done | bytes 196640 | tf_op jit(solution)/shard_map/ppermute | solution.py:131
  228.6 4.8 %collective-permute-done.54 = bf16[128,768]{1,0:T(8,128)(2,1)S(1)} collective-permute-done((bf16[128,768]{1,0:T(8,128)(2,1)S(1)}, bf16[128,768]{1,0:T(8,128)(2,1)S(1)}, u32[]{:S(2)}, u32[]{:S(2)}) %collective-permute-start.54) | collective-permute-done | bytes 196640 | tf_op jit(solution)/shard_map/ppermute | solution.py:131
  233.7 5.9 %shard_map.70 = (bf16[128,768]{1,0:T(8,128)(2,1)S(1)}, bf16[128,768]{1,0:T(8,128)(2,1)S(1)}) custom-call(bf16[128,768]{1,0:T(8,128)(2,1)S(1)} %add_convert_fusion.20.mine_ref, bf16[128,768]{1,0:T(8,128)(2,1)S(1)} %collective-permute-done.23.other_ref, f32[256,128]{1,0:T(8,128)S(1)} %broadcast_in_dim.19.mask_ref, f32[1,768]{1,0:T(1,128)S(1)} %copy-done.12, ...), custom_call_target="tpu_custom_call" | custom-call | flops 2415919104 | bytes 9437184 | tf_op jit(solution)/shard_map/pallas_call | solution.py:84
  240.1 5.7 %shard_map.78 = (bf16[128,768]{1,0:T(8,128)(2,1)S(1)}, bf16[128,768]{1,0:T(8,128)(2,1)S(1)}) custom-call(bf16[128,768]{1,0:T(8,128)(2,1)S(1)} %add_convert_fusion.4.mine_ref, bf16[128,768]{1,0:T(8,128)(2,1)S(1)} %collective-permute-done.55.other_ref, f32[256,128]{1,0:T(8,128)S(1)} %broadcast_in_dim.23.mask_ref, f32[1,768]{1,0:T(1,128)S(1)} %copy-done.12, ...), custom_call_target="tpu_custom_call" | custom-call | flops 2415919104 | bytes 9437184 | tf_op jit(solution)/shard_map/pallas_call | solution.py:84
  252.9 4.4 %collective-permute-done.26 = bf16[128,768]{1,0:T(8,128)(2,1)S(1)} collective-permute-done((bf16[128,768]{1,0:T(8,128)(2,1)S(1)}, bf16[128,768]{1,0:T(8,128)(2,1)S(1)}, u32[]{:S(2)}, u32[]{:S(2)}) %collective-permute-start.26) | collective-permute-done | bytes 196640 | tf_op jit(solution)/shard_map/ppermute | solution.py:131
  261.4 4.4 %collective-permute-done.58 = bf16[128,768]{1,0:T(8,128)(2,1)S(1)} collective-permute-done((bf16[128,768]{1,0:T(8,128)(2,1)S(1)}, bf16[128,768]{1,0:T(8,128)(2,1)S(1)}, u32[]{:S(2)}, u32[]{:S(2)}) %collective-permute-start.58) | collective-permute-done | bytes 196640 | tf_op jit(solution)/shard_map/ppermute | solution.py:131
  266.3 5.7 %shard_map.71 = (bf16[128,768]{1,0:T(8,128)(2,1)S(1)}, bf16[128,768]{1,0:T(8,128)(2,1)S(1)}) custom-call(bf16[128,768]{1,0:T(8,128)(2,1)S(1)} %add_convert_fusion.18.mine_ref, bf16[128,768]{1,0:T(8,128)(2,1)S(1)} %collective-permute-done.27.other_ref, f32[256,128]{1,0:T(8,128)S(1)} %broadcast_in_dim.19.mask_ref, f32[1,768]{1,0:T(1,128)S(1)} %copy-done.12, ...), custom_call_target="tpu_custom_call" | custom-call | flops 2415919104 | bytes 9437184 | tf_op jit(solution)/shard_map/pallas_call | solution.py:84
  272.2 5.7 %shard_map.79 = (bf16[128,768]{1,0:T(8,128)(2,1)S(1)}, bf16[128,768]{1,0:T(8,128)(2,1)S(1)}) custom-call(bf16[128,768]{1,0:T(8,128)(2,1)S(1)} %add_convert_fusion.2.mine_ref, bf16[128,768]{1,0:T(8,128)(2,1)S(1)} %collective-permute-done.59.other_ref, f32[256,128]{1,0:T(8,128)S(1)} %broadcast_in_dim.23.mask_ref, f32[1,768]{1,0:T(1,128)S(1)} %copy-done.12, ...), custom_call_target="tpu_custom_call" | custom-call | flops 2415919104 | bytes 9437184 | tf_op jit(solution)/shard_map/pallas_call | solution.py:84
  286.6 4.8 %collective-permute-done.30 = bf16[128,768]{1,0:T(8,128)(2,1)S(1)} collective-permute-done((bf16[128,768]{1,0:T(8,128)(2,1)S(1)}, bf16[128,768]{1,0:T(8,128)(2,1)S(1)}, u32[]{:S(2)}, u32[]{:S(2)}) %collective-permute-start.30) | collective-permute-done | bytes 196640 | tf_op jit(solution)/shard_map/ppermute | solution.py:131
  295.0 4.8 %collective-permute-done.62 = bf16[128,768]{1,0:T(8,128)(2,1)S(1)} collective-permute-done((bf16[128,768]{1,0:T(8,128)(2,1)S(1)}, bf16[128,768]{1,0:T(8,128)(2,1)S(1)}, u32[]{:S(2)}, u32[]{:S(2)}) %collective-permute-start.62) | collective-permute-done | bytes 196640 | tf_op jit(solution)/shard_map/ppermute | solution.py:131
  301.7 9.8 %collective-permute-done.64 = bf16[128,768]{1,0:T(8,128)(2,1)S(1)} collective-permute-done((bf16[128,768]{1,0:T(8,128)(2,1)S(1)}, bf16[128,768]{1,0:T(8,128)(2,1)S(1)}, u32[]{:S(2)}, u32[]{:S(2)}) %collective-permute-start.64) | collective-permute-done | bytes 196640 | tf_op jit(solution)/shard_map/ppermute | solution.py:131
  (197 shorter events, 136.2 us)
Async XLA Ops:
  26.6 11.3 %collective-permute-start = (bf16[128,768]{1,0:T(8,128)(2,1)S(1)}, bf16[128,768]{1,0:T(8,128)(2,1)S(1)}, u32[]{:S(2)}, u32[]{:S(2)}) collective-permute-start(bf16[128,768]{1,0:T(8,128)(2,1)S(1)} %get-tuple-element.38), channel_id=1, source_target_pairs={{0,1},{1,0},{2,3},{3,2},{4,5},{5,4},{6,7},{7,6},{8,9},{9,8},{10,11... | collective-permute-start | bytes 589832 | tf_op jit(solution)/shard_map/ppermute | solution.py:131
  39.5 10.0 %collective-permute-start.2 = (bf16[128,768]{1,0:T(8,128)(2,1)S(1)}, bf16[128,768]{1,0:T(8,128)(2,1)S(1)}, u32[]{:S(2)}, u32[]{:S(2)}) collective-permute-start(bf16[128,768]{1,0:T(8,128)(2,1)S(1)} %add_convert_fusion.31), channel_id=1, source_target_pairs={{0,7},{1,6},{2,5},{3,4},{4,3},{5,2},{6,1},{7,0},{8,15},{9,14},{10,... | collective-permute-start | bytes 589832 | tf_op jit(solution)/shard_map/ppermute | solution.py:131
  40.5 12.7 %collective-permute-start.33 = (bf16[128,768]{1,0:T(8,128)(2,1)S(1)}, bf16[128,768]{1,0:T(8,128)(2,1)S(1)}, u32[]{:S(2)}, u32[]{:S(2)}) collective-permute-start(bf16[128,768]{1,0:T(8,128)(2,1)S(1)} %add_convert_fusion.15), channel_id=1, source_target_pairs={{0,5},{1,4},{2,7},{3,6},{4,1},{5,0},{6,3},{7,2},{8,13},{9,12},{10,... | collective-permute-start | bytes 589832 | tf_op jit(solution)/shard_map/ppermute | solution.py:131
  42.0 15.9 %collective-permute-start.34 = (bf16[128,768]{1,0:T(8,128)(2,1)S(1)}, bf16[128,768]{1,0:T(8,128)(2,1)S(1)}, u32[]{:S(2)}, u32[]{:S(2)}) collective-permute-start(bf16[128,768]{1,0:T(8,128)(2,1)S(1)} %add_convert_fusion.15), channel_id=1, source_target_pairs={{0,7},{1,6},{2,5},{3,4},{4,3},{5,2},{6,1},{7,0},{8,15},{9,14},{10,... | collective-permute-start | bytes 589832 | tf_op jit(solution)/shard_map/ppermute | solution.py:131
  58.0 11.1 %collective-permute-start.35 = (bf16[128,768]{1,0:T(8,128)(2,1)S(1)}, bf16[128,768]{1,0:T(8,128)(2,1)S(1)}, u32[]{:S(2)}, u32[]{:S(2)}) collective-permute-start(bf16[128,768]{1,0:T(8,128)(2,1)S(1)} %add_convert_fusion.14.mine_ref), channel_id=1, source_target_pairs={{0,1},{1,0},{2,3},{3,2},{4,5},{5,4},{6,7},{7,6},{8,9},{9,8},{10,11... | collective-permute-start | bytes 589832 | tf_op jit(solution)/shard_map/ppermute | solution.py:131
  68.8 11.1 %collective-permute-start.4 = (bf16[128,768]{1,0:T(8,128)(2,1)S(1)}, bf16[128,768]{1,0:T(8,128)(2,1)S(1)}, u32[]{:S(2)}, u32[]{:S(2)}) collective-permute-start(bf16[128,768]{1,0:T(8,128)(2,1)S(1)} %get-tuple-element.40), channel_id=1, source_target_pairs={{0,1},{1,0},{2,3},{3,2},{4,5},{5,4},{6,7},{7,6},{8,9},{9,8},{10,11... | collective-permute-start | bytes 589832 | tf_op jit(solution)/shard_map/ppermute | solution.py:131
  81.2 11.1 %collective-permute-start.6 = (bf16[128,768]{1,0:T(8,128)(2,1)S(1)}, bf16[128,768]{1,0:T(8,128)(2,1)S(1)}, u32[]{:S(2)}, u32[]{:S(2)}) collective-permute-start(bf16[128,768]{1,0:T(8,128)(2,1)S(1)} %add_convert_fusion.29), channel_id=1, source_target_pairs={{0,3},{1,2},{2,1},{3,0},{4,11},{5,10},{6,9},{7,8},{8,7},{9,6},{10,... | collective-permute-start | bytes 589832 | tf_op jit(solution)/shard_map/ppermute | solution.py:131
  83.1 13.2 %collective-permute-start.37 = (bf16[128,768]{1,0:T(8,128)(2,1)S(1)}, bf16[128,768]{1,0:T(8,128)(2,1)S(1)}, u32[]{:S(2)}, u32[]{:S(2)}) collective-permute-start(bf16[128,768]{1,0:T(8,128)(2,1)S(1)} %add_convert_fusion.13), channel_id=1, source_target_pairs={{0,1},{1,0},{2,3},{3,2},{4,9},{5,8},{6,11},{7,10},{8,5},{9,4},{10,... | collective-permute-start | bytes 589832 | tf_op jit(solution)/shard_map/ppermute | solution.py:131
  84.3 16.5 %collective-permute-start.38 = (bf16[128,768]{1,0:T(8,128)(2,1)S(1)}, bf16[128,768]{1,0:T(8,128)(2,1)S(1)}, u32[]{:S(2)}, u32[]{:S(2)}) collective-permute-start(bf16[128,768]{1,0:T(8,128)(2,1)S(1)} %add_convert_fusion.13), channel_id=1, source_target_pairs={{0,3},{1,2},{2,1},{3,0},{4,11},{5,10},{6,9},{7,8},{8,7},{9,6},{10,... | collective-permute-start | bytes 589832 | tf_op jit(solution)/shard_map/ppermute | solution.py:131
  115.4 9.5 %collective-permute-start.9 = (bf16[128,768]{1,0:T(8,128)(2,1)S(1)}, bf16[128,768]{1,0:T(8,128)(2,1)S(1)}, u32[]{:S(2)}, u32[]{:S(2)}) collective-permute-start(bf16[128,768]{1,0:T(8,128)(2,1)S(1)} %add_convert_fusion.27), channel_id=1, source_target_pairs={{0,5},{1,4},{2,7},{3,6},{4,1},{5,0},{6,3},{7,2},{8,13},{9,12},{10,... | collective-permute-start | bytes 589832 | tf_op jit(solution)/shard_map/ppermute | solution.py:131
  115.8 13.3 %collective-permute-start.41 = (bf16[128,768]{1,0:T(8,128)(2,1)S(1)}, bf16[128,768]{1,0:T(8,128)(2,1)S(1)}, u32[]{:S(2)}, u32[]{:S(2)}) collective-permute-start(bf16[128,768]{1,0:T(8,128)(2,1)S(1)} %add_convert_fusion.11), channel_id=1, source_target_pairs={{0,5},{1,4},{2,7},{3,6},{4,1},{5,0},{6,3},{7,2},{8,13},{9,12},{10,... | collective-permute-start | bytes 589832 | tf_op jit(solution)/shard_map/ppermute | solution.py:131
  117.3 16.2 %collective-permute-start.42 = (bf16[128,768]{1,0:T(8,128)(2,1)S(1)}, bf16[128,768]{1,0:T(8,128)(2,1)S(1)}, u32[]{:S(2)}, u32[]{:S(2)}) collective-permute-start(bf16[128,768]{1,0:T(8,128)(2,1)S(1)} %add_convert_fusion.11), channel_id=1, source_target_pairs={{0,7},{1,6},{2,5},{3,4},{4,3},{5,2},{6,1},{7,0},{8,15},{9,14},{10,... | collective-permute-start | bytes 589832 | tf_op jit(solution)/shard_map/ppermute | solution.py:131
  124.9 9.1 %collective-permute-start.11 = (bf16[128,768]{1,0:T(8,128)(2,1)S(1)}, bf16[128,768]{1,0:T(8,128)(2,1)S(1)}, u32[]{:S(2)}, u32[]{:S(2)}) collective-permute-start(bf16[128,768]{1,0:T(8,128)(2,1)S(1)} %add_convert_fusion.26.mine_ref), channel_id=1, source_target_pairs={{0,1},{1,0},{2,3},{3,2},{4,5},{5,4},{6,7},{7,6},{8,9},{9,8},{10,11... | collective-permute-start | bytes 589832 | tf_op jit(solution)/shard_map/ppermute | solution.py:131
  147.6 11.5 %collective-permute-start.14 = (bf16[128,768]{1,0:T(8,128)(2,1)S(1)}, bf16[128,768]{1,0:T(8,128)(2,1)S(1)}, u32[]{:S(2)}, u32[]{:S(2)}) collective-permute-start(bf16[128,768]{1,0:T(8,128)(2,1)S(1)} %add_convert_fusion.25), channel_id=1, source_target_pairs={{0,3},{1,2},{2,1},{3,0},{4,11},{5,10},{6,9},{7,8},{8,7},{9,6},{10,... | collective-permute-start | bytes 589832 | tf_op jit(solution)/shard_map/ppermute | solution.py:131
  149.8 12.9 %collective-permute-start.45 = (bf16[128,768]{1,0:T(8,128)(2,1)S(1)}, bf16[128,768]{1,0:T(8,128)(2,1)S(1)}, u32[]{:S(2)}, u32[]{:S(2)}) collective-permute-start(bf16[128,768]{1,0:T(8,128)(2,1)S(1)} %add_convert_fusion.9), channel_id=1, source_target_pairs={{0,1},{1,0},{2,3},{3,2},{4,9},{5,8},{6,11},{7,10},{8,5},{9,4},{10,... | collective-permute-start | bytes 589832 | tf_op jit(solution)/shard_map/ppermute | solution.py:131
  151.0 16.5 %collective-permute-start.46 = (bf16[128,768]{1,0:T(8,128)(2,1)S(1)}, bf16[128,768]{1,0:T(8,128)(2,1)S(1)}, u32[]{:S(2)}, u32[]{:S(2)}) collective-permute-start(bf16[128,768]{1,0:T(8,128)(2,1)S(1)} %add_convert_fusion.9), channel_id=1, source_target_pairs={{0,3},{1,2},{2,1},{3,0},{4,11},{5,10},{6,9},{7,8},{8,7},{9,6},{10,... | collective-permute-start | bytes 589832 | tf_op jit(solution)/shard_map/ppermute | solution.py:131
  181.5 9.7 %collective-permute-start.18 = (bf16[128,768]{1,0:T(8,128)(2,1)S(1)}, bf16[128,768]{1,0:T(8,128)(2,1)S(1)}, u32[]{:S(2)}, u32[]{:S(2)}) collective-permute-start(bf16[128,768]{1,0:T(8,128)(2,1)S(1)} %add_convert_fusion.23), channel_id=1, source_target_pairs={{0,7},{1,6},{2,5},{3,4},{4,3},{5,2},{6,1},{7,0},{8,15},{9,14},{10,... | collective-permute-start | bytes 589832 | tf_op jit(solution)/shard_map/ppermute | solution.py:131
  182.2 13.0 %collective-permute-start.49 = (bf16[128,768]{1,0:T(8,128)(2,1)S(1)}, bf16[128,768]{1,0:T(8,128)(2,1)S(1)}, u32[]{:S(2)}, u32[]{:S(2)}) collective-permute-start(bf16[128,768]{1,0:T(8,128)(2,1)S(1)} %add_convert_fusion.7), channel_id=1, source_target_pairs={{0,5},{1,4},{2,7},{3,6},{4,1},{5,0},{6,3},{7,2},{8,13},{9,12},{10,... | collective-permute-start | bytes 589832 | tf_op jit(solution)/shard_map/ppermute | solution.py:131
  183.7 15.9 %collective-permute-start.50 = (bf16[128,768]{1,0:T(8,128)(2,1)S(1)}, bf16[128,768]{1,0:T(8,128)(2,1)S(1)}, u32[]{:S(2)}, u32[]{:S(2)}) collective-permute-start(bf16[128,768]{1,0:T(8,128)(2,1)S(1)} %add_convert_fusion.7), channel_id=1, source_target_pairs={{0,7},{1,6},{2,5},{3,4},{4,3},{5,2},{6,1},{7,0},{8,15},{9,14},{10,... | collective-permute-start | bytes 589832 | tf_op jit(solution)/shard_map/ppermute | solution.py:131
  191.2 8.9 %collective-permute-start.19 = (bf16[128,768]{1,0:T(8,128)(2,1)S(1)}, bf16[128,768]{1,0:T(8,128)(2,1)S(1)}, u32[]{:S(2)}, u32[]{:S(2)}) collective-permute-start(bf16[128,768]{1,0:T(8,128)(2,1)S(1)} %add_convert_fusion.22.mine_ref), channel_id=1, source_target_pairs={{0,1},{1,0},{2,3},{3,2},{4,5},{5,4},{6,7},{7,6},{8,9},{9,8},{10,11... | collective-permute-start | bytes 589832 | tf_op jit(solution)/shard_map/ppermute | solution.py:131
  213.5 11.5 %collective-permute-start.22 = (bf16[128,768]{1,0:T(8,128)(2,1)S(1)}, bf16[128,768]{1,0:T(8,128)(2,1)S(1)}, u32[]{:S(2)}, u32[]{:S(2)}) collective-permute-start(bf16[128,768]{1,0:T(8,128)(2,1)S(1)} %add_convert_fusion.21), channel_id=1, source_target_pairs={{0,3},{1,2},{2,1},{3,0},{4,11},{5,10},{6,9},{7,8},{8,7},{9,6},{10,... | collective-permute-start | bytes 589832 | tf_op jit(solution)/shard_map/ppermute | solution.py:131
  215.8 12.9 %collective-permute-start.53 = (bf16[128,768]{1,0:T(8,128)(2,1)S(1)}, bf16[128,768]{1,0:T(8,128)(2,1)S(1)}, u32[]{:S(2)}, u32[]{:S(2)}) collective-permute-start(bf16[128,768]{1,0:T(8,128)(2,1)S(1)} %add_convert_fusion.5), channel_id=1, source_target_pairs={{0,1},{1,0},{2,3},{3,2},{4,9},{5,8},{6,11},{7,10},{8,5},{9,4},{10,... | collective-permute-start | bytes 589832 | tf_op jit(solution)/shard_map/ppermute | solution.py:131
  216.9 16.5 %collective-permute-start.54 = (bf16[128,768]{1,0:T(8,128)(2,1)S(1)}, bf16[128,768]{1,0:T(8,128)(2,1)S(1)}, u32[]{:S(2)}, u32[]{:S(2)}) collective-permute-start(bf16[128,768]{1,0:T(8,128)(2,1)S(1)} %add_convert_fusion.5), channel_id=1, source_target_pairs={{0,3},{1,2},{2,1},{3,0},{4,11},{5,10},{6,9},{7,8},{8,7},{9,6},{10,... | collective-permute-start | bytes 589832 | tf_op jit(solution)/shard_map/ppermute | solution.py:131
  247.6 9.7 %collective-permute-start.26 = (bf16[128,768]{1,0:T(8,128)(2,1)S(1)}, bf16[128,768]{1,0:T(8,128)(2,1)S(1)}, u32[]{:S(2)}, u32[]{:S(2)}) collective-permute-start(bf16[128,768]{1,0:T(8,128)(2,1)S(1)} %add_convert_fusion.19), channel_id=1, source_target_pairs={{0,7},{1,6},{2,5},{3,4},{4,3},{5,2},{6,1},{7,0},{8,15},{9,14},{10,... | collective-permute-start | bytes 589832 | tf_op jit(solution)/shard_map/ppermute | solution.py:131
  248.3 13.0 %collective-permute-start.57 = (bf16[128,768]{1,0:T(8,128)(2,1)S(1)}, bf16[128,768]{1,0:T(8,128)(2,1)S(1)}, u32[]{:S(2)}, u32[]{:S(2)}) collective-permute-start(bf16[128,768]{1,0:T(8,128)(2,1)S(1)} %add_convert_fusion.3), channel_id=1, source_target_pairs={{0,5},{1,4},{2,7},{3,6},{4,1},{5,0},{6,3},{7,2},{8,13},{9,12},{10,... | collective-permute-start | bytes 589832 | tf_op jit(solution)/shard_map/ppermute | solution.py:131
  249.9 15.9 %collective-permute-start.58 = (bf16[128,768]{1,0:T(8,128)(2,1)S(1)}, bf16[128,768]{1,0:T(8,128)(2,1)S(1)}, u32[]{:S(2)}, u32[]{:S(2)}) collective-permute-start(bf16[128,768]{1,0:T(8,128)(2,1)S(1)} %add_convert_fusion.3), channel_id=1, source_target_pairs={{0,7},{1,6},{2,5},{3,4},{4,3},{5,2},{6,1},{7,0},{8,15},{9,14},{10,... | collective-permute-start | bytes 589832 | tf_op jit(solution)/shard_map/ppermute | solution.py:131
  279.9 11.5 %collective-permute-start.30 = (bf16[128,768]{1,0:T(8,128)(2,1)S(1)}, bf16[128,768]{1,0:T(8,128)(2,1)S(1)}, u32[]{:S(2)}, u32[]{:S(2)}) collective-permute-start(bf16[128,768]{1,0:T(8,128)(2,1)S(1)} %add_convert_fusion.17), channel_id=1, source_target_pairs={{0,3},{1,2},{2,1},{3,0},{4,11},{5,10},{6,9},{7,8},{8,7},{9,6},{10,... | collective-permute-start | bytes 589832 | tf_op jit(solution)/shard_map/ppermute | solution.py:131
  282.2 12.9 %collective-permute-start.61 = (bf16[128,768]{1,0:T(8,128)(2,1)S(1)}, bf16[128,768]{1,0:T(8,128)(2,1)S(1)}, u32[]{:S(2)}, u32[]{:S(2)}) collective-permute-start(bf16[128,768]{1,0:T(8,128)(2,1)S(1)} %add_convert_fusion.1), channel_id=1, source_target_pairs={{0,1},{1,0},{2,3},{3,2},{4,9},{5,8},{6,11},{7,10},{8,5},{9,4},{10,... | collective-permute-start | bytes 589832 | tf_op jit(solution)/shard_map/ppermute | solution.py:131
  283.4 16.5 %collective-permute-start.62 = (bf16[128,768]{1,0:T(8,128)(2,1)S(1)}, bf16[128,768]{1,0:T(8,128)(2,1)S(1)}, u32[]{:S(2)}, u32[]{:S(2)}) collective-permute-start(bf16[128,768]{1,0:T(8,128)(2,1)S(1)} %add_convert_fusion.1), channel_id=1, source_target_pairs={{0,3},{1,2},{2,1},{3,0},{4,11},{5,10},{6,9},{7,8},{8,7},{9,6},{10,... | collective-permute-start | bytes 589832 | tf_op jit(solution)/shard_map/ppermute | solution.py:131
  291.5 10.2 %collective-permute-start.31 = (bf16[128,768]{1,0:T(8,128)(2,1)S(1)}, bf16[128,768]{1,0:T(8,128)(2,1)S(1)}, u32[]{:S(2)}, u32[]{:S(2)}) collective-permute-start(bf16[128,768]{1,0:T(8,128)(2,1)S(1)} %add_convert_fusion.16), channel_id=1, source_target_pairs={{0,1},{1,0},{2,3},{3,2},{4,5},{5,4},{6,7},{7,6},{8,9},{9,8},{10,11... | collective-permute-start | bytes 589832 | tf_op jit(solution)/shard_map/ppermute | solution.py:131
  300.1 11.5 %collective-permute-start.64 = (bf16[128,768]{1,0:T(8,128)(2,1)S(1)}, bf16[128,768]{1,0:T(8,128)(2,1)S(1)}, u32[]{:S(2)}, u32[]{:S(2)}) collective-permute-start(bf16[128,768]{1,0:T(8,128)(2,1)S(1)} %pad_maximum_fusion), channel_id=1, source_target_pairs={{0,4},{1,5},{2,6},{3,7},{4,0},{5,1},{6,2},{7,3},{8,12},{9,13},{10,... | collective-permute-start | bytes 589832 | tf_op jit(solution)/shard_map/ppermute | solution.py:131
  301.7 9.9 %collective-permute-start.65 = (bf16[128,768]{1,0:T(8,128)(2,1)S(1)}, bf16[128,768]{1,0:T(8,128)(2,1)S(1)}, u32[]{:S(2)}, u32[]{:S(2)}) collective-permute-start(bf16[128,768]{1,0:T(8,128)(2,1)S(1)} %pad_maximum_fusion), channel_id=1, source_target_pairs={{0,1},{1,0},{2,3},{3,2},{4,8},{5,9},{6,10},{7,11},{8,4},{9,5},{10,... | collective-permute-start | bytes 589832 | tf_op jit(solution)/shard_map/ppermute | solution.py:131
  (47 other events, 303.3 us)
